TPU v7x, 32 devices: a whole 2x2x4 slice. The times are simulated.
32 devices in a mesh: group: 2 (over y), batch: 4 (over z), expert: 4 (over x, core).
Axes of the slice: x: 2, y: 2, z: 4, core: 2. Of those that a mesh axis runs over, the one named last changes fastest.
Arguments:
- residual_in: bfloat16 [128, 4096], P(('group', 'batch')), parts along dimension 0, may hold values from -11 to 11
- queries: bfloat16 [128, 16, 128], P(('group', 'batch'), 'expert'), parts along dimension 0, may hold values from -150 to 150
- key_new: bfloat16 [128, 4, 128], P(('group', 'batch'), 'expert'), parts along dimension 0, may hold values from -6 to 6
- value_new: bfloat16 [128, 4, 128], P(('group', 'batch'), 'expert'), parts along dimension 0, may hold values from -6 to 6
- key_cache: bfloat16 [128, 4, 256, 128], P(('group', 'batch'), 'expert'), parts along dimension 0, may hold values from -6 to 6
- value_cache: bfloat16 [128, 4, 256, 128], P(('group', 'batch'), 'expert'), parts along dimension 0, may hold values from -6 to 6
- cache_len: int32 [128], P(('group', 'batch')), parts along dimension 0, may hold values from 1 to 256, 8192 in all
- new_slot: int32 [128], P(('group', 'batch')), parts along dimension 0, may hold values 0 or 1
- out_weight: bfloat16 [2048, 4096], P('expert'), may hold values from -0.125 to 0.125
- norm_gain: float32 [4096], replicated, may hold values from 0.5 to 1.5
- router: bfloat16 [4096, 4], replicated, may hold values from -0.09375 to 0.09375
- chosen: int32 [128, 2], P(('group', 'batch')), parts along dimension 0, may hold values from 0 to 3, all different within a row; in each aligned block of 16 rows (0 to 15, 16 to 31, ...) at most 12 rows name the same one
- w_gate: bfloat16 [4, 4096, 8192], P('expert', None, 'batch'), may hold values from -0.09375 to 0.09375
- w_up: bfloat16 [4, 4096, 8192], P('expert', None, 'batch'), may hold values from -0.09375 to 0.09375
- w_down: bfloat16 [4, 8192, 4096], P('expert', 'batch'), may hold values from -0.0625 to 0.0625
Outputs:
- layer_out: bfloat16 [128, 4096], P(('group', 'batch', 'expert')), parts along dimension 0
There are 2 independent parts, one for each index of `group`. A program takes and returns all parts, laid end to end along the dimension named above; an argument that names none is the same for every part. Nothing has to cross between parts.
Inputs may be any that keep to these rules, and one draw needn't show every extreme that they name: `chosen`: each row names 2 different experts. Among the rows of one device no expert is named by more than 12 rows, and in every draw some expert is named by exactly 12 rows of some device. `cache_len`: the lengths of a part sum to 8192, and the largest is exactly 256.
All inputs are finite; a program needn't handle non-finite values. No bound on the sum of `cache_len` or of `new_slot` on one device may be relied on, other than what follows from the above.
Results may differ from a plain program's by a relative error of at most 0.017.
Values may be sent and summed in bfloat16 or wider, within the bound.
No kernel may reach another device: no remote copies, remote signals or barrier semaphores. Data moves between devices by JAX's collectives and lax.ppermute only.
A program may use at most 128 MiB of HBM per device.

v0:
```python
import jax
import jax.numpy as jnp
from jax import lax
from jax.sharding import PartitionSpec as P

CAP = 12
epsilon = 1e-05


def attend(queries, key_new, value_new, key_cache, value_cache, cache_len, new_slot):
    slot_count, kv_count, length, head_width = key_cache.shape
    group_size = queries.shape[1] // kv_count
    grouped = queries.reshape(slot_count, kv_count, group_size, head_width)
    scaling = float(head_width) ** (-0.5)
    scores = (
        jnp.einsum("skgd,sktd->skgt", grouped, key_cache, preferred_element_type=jnp.float32)
        * scaling
    )
    own_score = (
        jnp.einsum("skgd,skd->skg", grouped, key_new, preferred_element_type=jnp.float32) * scaling
    )
    places = lax.broadcasted_iota(jnp.int32, (slot_count, length), 1)
    usable = (places < cache_len[:, None]) & (new_slot[:, None] == 0)
    usable = usable[:, None, None, :]
    scores = jnp.where(usable, scores, jnp.float32(-1e30))
    highest = jnp.maximum(jnp.max(scores, axis=3), own_score)
    weights = jnp.where(usable, jnp.exp(scores - highest[..., None]), jnp.float32(0.0))
    own_weight = jnp.exp(own_score - highest)
    denominator = jnp.sum(weights, axis=3) + own_weight
    probabilities = (weights / denominator[..., None]).astype(jnp.bfloat16)
    own_prob = (own_weight / denominator).astype(jnp.bfloat16)
    attended = jnp.einsum(
        "skgt,sktd->skgd", probabilities, value_cache, preferred_element_type=jnp.float32
    )
    attended = (
        attended
        + own_prob.astype(jnp.float32)[..., None] * value_new.astype(jnp.float32)[:, :, None, :]
    )
    return attended.reshape(slot_count, kv_count * group_size * head_width).astype(jnp.bfloat16)


def mixing(logits, chosen, expert_count):
    labels = lax.broadcasted_iota(jnp.int32, (1, 1, expert_count), 2)
    picking = (chosen[:, :, None] == labels).astype(jnp.float32)
    chosen_logits = jnp.sum(picking * logits[:, None, :], axis=2)
    leading = jax.nn.sigmoid(chosen_logits[:, 0] - chosen_logits[:, 1])
    fractions = jnp.stack([leading, 1.0 - leading], axis=1)
    return jnp.sum(picking * fractions[:, :, None], axis=1)


def placement_table(chosen, targets, capacity):
    routed = jnp.sum((chosen[None, :, :] == targets[:, None, None]).astype(jnp.int32), axis=2)
    position = jnp.cumsum(routed, axis=1) - routed
    row_labels = lax.broadcasted_iota(jnp.int32, (1, capacity, 1), 1)
    return ((position[:, None, :] == row_labels) & (routed[:, None, :] == 1)).astype(jnp.float32)


def body(
    residual_in,
    queries,
    key_new,
    value_new,
    key_cache,
    value_cache,
    cache_len,
    new_slot,
    out_weight,
    norm_gain,
    router,
    chosen,
    w_gate,
    w_up,
    w_down,
):
    my_expert = lax.axis_index("expert")
    attended = attend(queries, key_new, value_new, key_cache, value_cache, cache_len, new_slot)
    partial_value = jnp.dot(attended, out_weight, preferred_element_type=jnp.float32)
    summed = lax.psum(partial_value, "expert")
    stream = (residual_in.astype(jnp.float32) + summed).astype(jnp.bfloat16)
    values = stream.astype(jnp.float32)
    scaling = lax.rsqrt(jnp.mean(values * values, axis=1, keepdims=True) + epsilon)
    normed = (values * scaling * norm_gain).astype(jnp.bfloat16)
    logits = jnp.dot(normed, router, preferred_element_type=jnp.float32)
    placing = placement_table(chosen, jnp.reshape(my_expert, (1,)), CAP)[0]
    sent_rows = jnp.dot(
        placing.astype(jnp.bfloat16), normed, preferred_element_type=jnp.float32
    ).astype(jnp.bfloat16)
    carried = values * (my_expert == 0).astype(jnp.float32)
    coef = mixing(logits, chosen, router.shape[1])
    expert_labels = lax.broadcasted_iota(jnp.int32, (1, router.shape[1]), 1)
    my_coef = jnp.sum(coef * (expert_labels == my_expert).astype(jnp.float32), axis=1)
    row_weight = jnp.dot(placing, my_coef, precision=lax.Precision.HIGHEST)
    block_rows = lax.all_gather(sent_rows, "batch", axis=0, tiled=True)
    gate_part = jnp.dot(block_rows, w_gate[0], preferred_element_type=jnp.float32)
    up_part = jnp.dot(block_rows, w_up[0], preferred_element_type=jnp.float32)
    hidden = (jax.nn.silu(gate_part) * up_part).astype(jnp.bfloat16)
    block_rows = hidden
    outputs = lax.psum_scatter(
        jnp.dot(block_rows, w_down[0], preferred_element_type=jnp.float32).astype(jnp.bfloat16),
        "batch",
        scatter_dimension=0,
        tiled=True,
    ).astype(jnp.float32)
    weighted = row_weight[:, None] * outputs
    contribution = jnp.dot(placing.T, weighted, precision=lax.Precision.HIGHEST) + carried
    layer_out = lax.psum_scatter(
        contribution.astype(jnp.bfloat16), "expert", scatter_dimension=0, tiled=True
    )
    return layer_out


def solution(mesh):
    in_specs = (
        P(("group", "batch"), None),
        P(("group", "batch"), "expert", None),
        P(("group", "batch"), "expert", None),
        P(("group", "batch"), "expert", None),
        P(("group", "batch"), "expert", None, None),
        P(("group", "batch"), "expert", None, None),
        P(("group", "batch")),
        P(("group", "batch")),
        P("expert", None),
        P(),
        P(),
        P(("group", "batch"), None),
        P("expert", None, "batch"),
        P("expert", None, "batch"),
        P("expert", "batch", None),
    )
    out_specs = P(("group", "batch", "expert"), None)
    return jax.shard_map(body, mesh=mesh, in_specs=in_specs, out_specs=out_specs, check_vma=False)
```

profile of v0, /device:TPU:0, one launch (start us, length us, event | category | flops | bytes accessed | tf_op | source)
XLA Modules:
  0.0 154.4 jit_solution(7242869067965577408)
XLA Ops:
  6.5 0.0 copy-start
  6.5 0.0 all-reduce.6.cloned.1.call-start
  6.5 0.7 broadcast_compare_fusion
  7.3 0.7 fusion.48
  8.0 0.9 fusion.52
  8.9 0.0 copy-done
  8.9 1.2 fusion.67
  10.1 0.2 fusion.37
  10.3 0.7 bitcast_convert_fusion
  11.0 1.5 fusion.19
  12.5 3.6 %fusion.45 = f32[16,4096]{1,0:T(8,128)} fusion(bf16[512,4096]{1,0:T(8,128)(2,1)} %param.23, bf16[2,8,4,128]{3,2,1,0:T(4,128)(2,1)S(1)} %bitcast.56), kind=kOutput, calls=%fused_computation.45 | convolution fusion | flops 67108864 | bytes 4472832 | tf_op jit(solution)/shard_map/dot_general | solution.py:77
  16.1 0.0 all-reduce.6.cloned.1.call-update
  16.1 0.0 all-reduce.8.cloned.1.call-start
  16.1 0.7 fusion.63
  16.8 0.1 copy.26
  17.0 0.1 reduce.6
  17.1 1.2 dynamic-slice.6
  19.0 32.2 %all-reduce.6.cloned.1.call-done = f32[16,4096]{1,0:T(8,128)} async-done(((f32[16,4096]{1,0:T(8,128)}), f32[16,4096]{1,0:T(8,128)}) %all-reduce.6.cloned.1.call-update) | async-done | bytes 262160 | tf_op jit(solution)/shard_map/psum | solution.py:78
  51.2 1.1 fusion.29
  52.4 1.0 fusion.11
  53.3 15.2 %all-gather = bf16[4,12,4096]{2,1,0:T(8,128)(2,1)S(1)} all-gather(bf16[1,12,4096]{2,1,0:T(8,128)(2,1)S(1)} %fusion.11), channel_id=1, replica_groups=mesh['group'=2,'batch'=4,'expert'=4] {'batch'}, dimensions={0}, use_global_device_ids=true | all-gather | bytes 491520 | tf_op jit(solution)/shard_map/all_gather | solution.py:93
  68.5 0.1 reshape.221
  68.6 8.8 %fusion.5 = f32[48,2048]{1,0:T(8,128)S(1)} fusion(bf16[48,4096]{1,0:T(8,128)(2,1)S(1)} %reshape.221, bf16[1,4096,2048]{2,1,0:T(8,128)(2,1)} %param.27), kind=kOutput, calls=%fused_computation.4 | convolution fusion | flops 805306368 | bytes 17563648 | tf_op jit(solution)/shard_map/dot_general | solution.py:94
  77.4 0.0 copy-start.1
  77.4 0.0 copy-start.3
  77.4 0.0 copy-start.2
  77.4 0.0 copy-start.4
  77.5 13.7 %fusion.7 = bf16[48,4096]{1,0:T(8,128)(2,1)S(1)} fusion(bf16[1,2048,4096]{2,1,0:T(8,128)(2,1)} %param.29, bf16[48,4096]{1,0:T(8,128)(2,1)S(1)} %reshape.221, bf16[1,4096,2048]{2,1,0:T(8,128)(2,1)} %param.28, f32[48,2048]{1,0:T(8,128)S(1)} %fusion.5), kind=kOutput, calls=%fused_computation.6 | convolution fusion | flops 1611399168 | bytes 34734080 | tf_op jit(solution)/shard_map/dot_general | solution.py:99
  91.1 16.0 %fusion = bf16[16,4096]{1,0:T(8,128)(2,1)S(1)} fusion(bf16[48,4096]{1,0:T(8,128)(2,1)S(1)} %fusion.7), kind=kCustom, calls=%all-reduce-scatter | all-reduce-scatter fusion | flops 262145 | bytes 524800
  107.2 2.8 %collective-permute-start = (bf16[12,4096]{1,0:T(8,128)(2,1)S(1)}, bf16[12,4096]{1,0:T(8,128)(2,1)S(1)}, u32[]{:S(2)}, u32[]{:S(2)}) collective-permute-start(bf16[12,4096]{1,0:T(8,128)(2,1)S(1)} %slice.8), channel_id=1, source_target_pairs={{0,4},{4,8},{8,12},{1,5},{5,9},{9,13},{2,6},{6,10},{10,14},{3,7},{... | collective-permute-start | bytes 294920
  110.0 0.0 copy-done.1
  110.1 0.0 copy-done.3
  110.1 0.2 fusion.43
  110.3 0.0 copy-done.2
  110.4 0.1 multiply_reduce_fusion
  110.5 0.1 convolution_bitcast_fusion
  110.6 2.0 %collective-permute-done = bf16[12,4096]{1,0:T(8,128)(2,1)S(1)} collective-permute-done((bf16[12,4096]{1,0:T(8,128)(2,1)S(1)}, bf16[12,4096]{1,0:T(8,128)(2,1)S(1)}, u32[]{:S(2)}, u32[]{:S(2)}) %collective-permute-start) | collective-permute-done | bytes 98336
  112.5 0.3 concatenate
  112.9 1.0 fusion.10
  113.9 0.0 all-reduce.8.cloned.1.call-update
  113.9 0.0 copy-done.4
  113.9 0.6 dynamic-slice.2
  115.1 31.0 %all-reduce.8.cloned.1.call-done = bf16[16,4096]{1,0:T(8,128)(2,1)} async-done(((bf16[16,4096]{1,0:T(8,128)(2,1)}), bf16[16,4096]{1,0:T(8,128)(2,1)}) %all-reduce.8.cloned.1.call-update) | async-done | bytes 131088
  146.1 1.5 constant_dynamic-slice_fusion
  (12 shorter events, 0.2 us)
Async XLA Ops:
  6.5 2.3 %copy-start = (bf16[16,1,256,128]{3,2,1,0:T(8,128)(2,1)S(1)}, bf16[16,1,256,128]{3,2,1,0:T(8,128)(2,1)}, u32[]{:S(2)}) copy-start(bf16[16,1,256,128]{3,2,1,0:T(8,128)(2,1)} %param.19) | copy-start | bytes 3145732
  6.5 44.7 %all-reduce.6.cloned.1.call-start = ((), (), s32[]{:S(2)}) async-start(), calls=%async_computation | async-start | bytes 524288 | tf_op jit(solution)/shard_map/psum | solution.py:78
  16.1 130.0 %all-reduce.8.cloned.1.call-start = ((), (), s32[]{:S(2)}) async-start(), calls=%async_computation.1 | async-start | bytes 262144
  77.4 32.6 %copy-start.1 = (f32[4096]{0:T(1024)S(1)}, f32[4096]{0:T(1024)}, u32[]{:S(2)}) copy-start(f32[4096]{0:T(1024)} %param.24) | copy-start | bytes 49156
  77.4 32.6 %copy-start.3 = (bf16[4096,4]{0,1:T(4,128)(2,1)S(1)}, bf16[4096,4]{0,1:T(4,128)(2,1)}, u32[]{:S(2)}) copy-start(bf16[4096,4]{0,1:T(4,128)(2,1)} %param.25) | copy-start | bytes 98308
  77.4 32.9 %copy-start.2 = (s32[16,2]{0,1:T(2,128)S(1)}, s32[16,2]{0,1:T(2,128)}, u32[]{:S(2)}) copy-start(s32[16,2]{0,1:T(2,128)} %param.26) | copy-start | bytes 388
  77.4 36.4 %copy-start.4 = (u32[32]{0:T(128)S(1)}, u32[32]{0:T(128)}, u32[]{:S(2)}) copy-start(u32[32]{0:T(128)} %constant.45) | copy-start | bytes 388
  107.2 5.4 %collective-permute-start = (bf16[12,4096]{1,0:T(8,128)(2,1)S(1)}, bf16[12,4096]{1,0:T(8,128)(2,1)S(1)}, u32[]{:S(2)}, u32[]{:S(2)}) collective-permute-start(bf16[12,4096]{1,0:T(8,128)(2,1)S(1)} %slice.8), channel_id=1, source_target_pairs={{0,4},{4,8},{8,12},{1,5},{5,9},{9,13},{2,6},{6,10},{10,14},{3,7},{... | collective-permute-start | bytes 294920
Sparse Core Ops, SparseCore 0:
  16.2 34.9 all-reduce.5
  114.0 32.0 all-reduce.7
where the time goes:
time: 155 us; the launch traced here: 154 us
  waiting for transfers between devices  65.2 us (42%)
  matrix products  31.9 us (21%)
  blocking collectives  31.2 us (20%)
  between operations  14.9 us (10%)
  other arithmetic  4.53 us (3%)
  local copies, waits for them, and re-layouts  3.85 us (2%)
  starting transfers between devices  2.89 us (2%)
    unnamed x4, waiting for transfers between devices  33 us
    psum x1, waiting for transfers between devices, body(): summed = lax.psum(partial_value, 'expert')  32.2 us
    unnamed x1, blocking collectives  16 us
    all_gather x1, blocking collectives, body(): block_rows = lax.all_gather(sent_rows, 'batch', axis=0, tiled=True)  15.2 us
    dot_general x1, matrix products, body(): jnp.dot(block_rows, w_down[0], preferred_element_type=jnp.float32)  13.7 us
    dot_general x1, matrix products, body(): jnp.dot(block_rows, w_gate[0], preferred_element_type=jnp.float32)  8.79 us
    unnamed x16, local copies, waits for them, and re-layouts  3.76 us
    dot_general x1, matrix products, body(): jnp.dot(attended, out_weight, preferred_element_type=jnp.float32)  3.56 us
  transfers between devices with their start and end apart: 3, of which 3 were waited for; matrix products, arithmetic and copies ran while one was open for 2% of the time, Pallas kernels for 0%

commit v1 on v0

--- a/solution.py
+++ b/solution.py
@@ -75,7 +75,7 @@
     my_expert = lax.axis_index("expert")
     attended = attend(queries, key_new, value_new, key_cache, value_cache, cache_len, new_slot)
     partial_value = jnp.dot(attended, out_weight, preferred_element_type=jnp.float32)
-    summed = lax.psum(partial_value, "expert")
+    summed = jnp.sum(lax.all_gather(partial_value, "expert"), axis=0)
     stream = (residual_in.astype(jnp.float32) + summed).astype(jnp.bfloat16)
     values = stream.astype(jnp.float32)
     scaling = lax.rsqrt(jnp.mean(values * values, axis=1, keepdims=True) + epsilon)

time: 155 us -> 141 us (0.910)
  waiting for transfers between devices: 65.2 us -> 48.8 us
  blocking collectives: 31.2 us -> 33.8 us
  starting transfers between devices: 2.89 us -> 1.34 us
    psum x1 -> x0, waiting for transfers between devices: 32.2 us -> none  [body(): summed = lax.psum(partial_value, 'expert')]
    all_gather x0 -> x1, waiting for transfers between devices: none -> 16.6 us  [body(): summed = jnp.sum(lax.all_gather(partial_value, 'expert'), axis=0)]
    unnamed x1, blocking collectives: 16 us -> 17.8 us
    unnamed x2, starting transfers between devices: 2.89 us -> 1.34 us
where the time goes in v1:
time: 141 us; the launch traced here: 140 us
  waiting for transfers between devices  48.8 us (35%)
  blocking collectives  33.8 us (24%)
  matrix products  31.9 us (23%)
  between operations  14.9 us (11%)
  other arithmetic  5.76 us (4%)
  local copies, waits for them, and re-layouts  3.85 us (3%)
    unnamed x4, waiting for transfers between devices  32.2 us
    unnamed x1, blocking collectives  17.8 us
    all_gather x1, waiting for transfers between devices, body(): summed = jnp.sum(lax.all_gather(partial_value, 'expert'), axis=0)  16.6 us
    all_gather x1, blocking collectives, body(): block_rows = lax.all_gather(sent_rows, 'batch', axis=0, tiled=True)  16 us
    dot_general x1, matrix products, body(): jnp.dot(block_rows, w_down[0], preferred_element_type=jnp.float32)  13.7 us
    dot_general x1, matrix products, body(): jnp.dot(block_rows, w_gate[0], preferred_element_type=jnp.float32)  8.79 us
    unnamed x16, local copies, waits for them, and re-layouts  3.76 us
    dot_general x1, matrix products, body(): jnp.dot(attended, out_weight, preferred_element_type=jnp.float32)  3.58 us
  transfers between devices with their start and end apart: 3, of which 3 were waited for; matrix products, arithmetic and copies ran while one was open for 2% of the time, Pallas kernels for 0%

profile of v1, /device:TPU:0, one launch (start us, length us, event | category | flops | bytes accessed | tf_op | source)
XLA Modules:
  0.0 140.4 jit_solution(12201496424224028612)
XLA Ops:
  6.5 0.0 copy-start
  6.5 0.0 all-gather.4.cloned.1.call-start
  6.5 0.7 broadcast_compare_fusion
  7.3 0.7 fusion.48
  8.0 0.9 fusion.52
  8.9 0.0 copy-done
  8.9 1.2 fusion.67
  10.1 0.2 fusion.37
  10.3 0.7 bitcast_convert_fusion
  11.0 1.5 %fusion.19 = bf16[16,4,128]{2,1,0:T(4,128)(2,1)S(1)} fusion(bf16[16,1,256,128]{3,2,1,0:T(8,128)(2,1)} %param.20, f32[16,4,256]{2,1,0:T(4,128)S(1)} %get-tuple-element.12, f32[16,4]{1,0:T(8,128)S(1)} %get-tuple-element.10, f32[16,4]{1,0:T(8,128)S(1)} %multiply_maximum_fusion, pred[16,256]{1,0:T(8,128)(4,1)S(1)} %fusion.48, ...), kind=kOutput, calls=%fused_computation.16 | convolution fusion | flops 4284416 | bytes 1143552 | tf_op jit(solution)/shard_map/skgt,sktd->skgd/dot_general | solution.py:32
  12.5 3.6 %fusion.45 = f32[16,4096]{1,0:T(8,128)} fusion(bf16[512,4096]{1,0:T(8,128)(2,1)} %param.23, bf16[2,8,4,128]{3,2,1,0:T(4,128)(2,1)S(1)} %bitcast.58), kind=kOutput, calls=%fused_computation.45 | convolution fusion | flops 67108864 | bytes 4472832 | tf_op jit(solution)/shard_map/dot_general | solution.py:77
  16.1 0.0 all-gather.4.cloned.1.call-update
  16.1 0.0 all-reduce.5.cloned.1.call-start
  16.2 0.7 fusion.63
  16.9 0.1 copy.26
  17.0 0.1 reduce.6
  17.1 1.2 dynamic-slice.6
  19.0 16.6 %all-gather.4.cloned.1.call-done = f32[64,4096]{1,0:T(8,128)} async-done(((f32[16,4096]{1,0:T(8,128)}), f32[64,4096]{1,0:T(8,128)}) %all-gather.4.cloned.1.call-update) | async-done | bytes 1048592 | tf_op jit(solution)/shard_map/all_gather | solution.py:78
  35.7 1.3 reduce_sum.65
  37.0 1.1 fusion.29
  38.1 1.0 fusion.11
  39.0 16.0 %all-gather.1 = bf16[4,12,4096]{2,1,0:T(8,128)(2,1)S(1)} all-gather(bf16[1,12,4096]{2,1,0:T(8,128)(2,1)S(1)} %fusion.11), channel_id=1, replica_groups=mesh['group'=2,'batch'=4,'expert'=4] {'batch'}, dimensions={0}, use_global_device_ids=true | all-gather | bytes 491520 | tf_op jit(solution)/shard_map/all_gather | solution.py:93
  55.0 0.1 reshape.222
  55.1 8.8 %fusion.5 = f32[48,2048]{1,0:T(8,128)S(1)} fusion(bf16[48,4096]{1,0:T(8,128)(2,1)S(1)} %reshape.222, bf16[1,4096,2048]{2,1,0:T(8,128)(2,1)} %param.27), kind=kOutput, calls=%fused_computation.4 | convolution fusion | flops 805306368 | bytes 17563648 | tf_op jit(solution)/shard_map/dot_general | solution.py:94
  63.9 0.0 copy-start.1
  63.9 0.0 copy-start.3
  63.9 0.0 copy-start.2
  63.9 0.0 copy-start.4
  64.0 13.7 %fusion.7 = bf16[48,4096]{1,0:T(8,128)(2,1)S(1)} fusion(bf16[1,2048,4096]{2,1,0:T(8,128)(2,1)} %param.29, bf16[48,4096]{1,0:T(8,128)(2,1)S(1)} %reshape.222, bf16[1,4096,2048]{2,1,0:T(8,128)(2,1)} %param.28, f32[48,2048]{1,0:T(8,128)S(1)} %fusion.5), kind=kOutput, calls=%fused_computation.6 | convolution fusion | flops 1611399168 | bytes 34734080 | tf_op jit(solution)/shard_map/dot_general | solution.py:99
  77.6 17.8 %fusion = bf16[16,4096]{1,0:T(8,128)(2,1)S(1)} fusion(bf16[48,4096]{1,0:T(8,128)(2,1)S(1)} %fusion.7), kind=kCustom, calls=%all-reduce-scatter | all-reduce-scatter fusion | flops 262145 | bytes 524800
  95.5 1.3 collective-permute-start
  96.8 0.0 copy-done.1
  96.8 0.0 copy-done.3
  96.8 0.2 fusion.43
  97.1 0.0 copy-done.2
  97.1 0.1 multiply_reduce_fusion
  97.2 0.1 convolution_bitcast_fusion
  97.4 2.0 %collective-permute-done = bf16[12,4096]{1,0:T(8,128)(2,1)S(1)} collective-permute-done((bf16[12,4096]{1,0:T(8,128)(2,1)S(1)}, bf16[12,4096]{1,0:T(8,128)(2,1)S(1)}, u32[]{:S(2)}, u32[]{:S(2)}) %collective-permute-start) | collective-permute-done | bytes 98336
  99.3 0.3 concatenate
  99.6 1.0 fusion.10
  100.6 0.0 all-reduce.5.cloned.1.call-update
  100.7 0.0 copy-done.4
  100.7 0.6 dynamic-slice.2
  101.9 30.2 %all-reduce.5.cloned.1.call-done = bf16[16,4096]{1,0:T(8,128)(2,1)} async-done(((bf16[16,4096]{1,0:T(8,128)(2,1)}), bf16[16,4096]{1,0:T(8,128)(2,1)}) %all-reduce.5.cloned.1.call-update) | async-done | bytes 131088
  132.1 1.5 %constant_dynamic-slice_fusion = bf16[4,4096]{1,0:T(4,128)(2,1)} fusion(bf16[16,4096]{1,0:T(8,128)(2,1)} %all-reduce.5.cloned.1.call-done, u32[]{:T(128)S(6)} %multiply.9), kind=kLoop, calls=%fused_computation.76 | loop fusion | bytes 65540
  (12 shorter events, 0.2 us)
Async XLA Ops:
  6.5 2.3 %copy-start = (bf16[16,1,256,128]{3,2,1,0:T(8,128)(2,1)S(1)}, bf16[16,1,256,128]{3,2,1,0:T(8,128)(2,1)}, u32[]{:S(2)}) copy-start(bf16[16,1,256,128]{3,2,1,0:T(8,128)(2,1)} %param.19) | copy-start | bytes 3145732
  6.5 29.1 %all-gather.4.cloned.1.call-start = ((), (), s32[]{:S(2)}) async-start(), calls=%async_computation | async-start | bytes 1310720 | tf_op jit(solution)/shard_map/all_gather | solution.py:78
  16.1 116.0 %all-reduce.5.cloned.1.call-start = ((), (), s32[]{:S(2)}) async-start(), calls=%async_computation.1 | async-start | bytes 262144
  63.9 32.9 %copy-start.1 = (f32[4096]{0:T(1024)S(1)}, f32[4096]{0:T(1024)}, u32[]{:S(2)}) copy-start(f32[4096]{0:T(1024)} %param.24) | copy-start | bytes 49156
  63.9 32.9 %copy-start.3 = (bf16[4096,4]{0,1:T(4,128)(2,1)S(1)}, bf16[4096,4]{0,1:T(4,128)(2,1)}, u32[]{:S(2)}) copy-start(bf16[4096,4]{0,1:T(4,128)(2,1)} %param.25) | copy-start | bytes 98308
  63.9 33.1 %copy-start.2 = (s32[16,2]{0,1:T(2,128)S(1)}, s32[16,2]{0,1:T(2,128)}, u32[]{:S(2)}) copy-start(s32[16,2]{0,1:T(2,128)} %param.26) | copy-start | bytes 388
  63.9 36.7 %copy-start.4 = (u32[32]{0:T(128)S(1)}, u32[32]{0:T(128)}, u32[]{:S(2)}) copy-start(u32[32]{0:T(128)} %constant.45) | copy-start | bytes 388
  95.5 3.8 %collective-permute-start = (bf16[12,4096]{1,0:T(8,128)(2,1)S(1)}, bf16[12,4096]{1,0:T(8,128)(2,1)S(1)}, u32[]{:S(2)}, u32[]{:S(2)}) collective-permute-start(bf16[12,4096]{1,0:T(8,128)(2,1)S(1)} %slice.8), channel_id=1, source_target_pairs={{0,4},{4,8},{8,12},{1,5},{5,9},{9,13},{2,6},{6,10},{10,14},{3,7},{... | collective-permute-start | bytes 294920
Sparse Core Ops, SparseCore 0:
  16.2 19.4 all-gather.3
  100.8 31.2 all-reduce.4
